TPU v7x, 32 devices: a whole 2x2x4 slice. The times are simulated.
32 devices in a mesh: blk: 8 (over y, x, core), row: 4 (over z).
Axes of the slice: x: 2, y: 2, z: 4, core: 2. Of those that a mesh axis runs over, the one named last changes fastest.
Arguments:
- rank_start: float32 [512, 128], P(('blk', 'row')), may hold values from 0.5 to 1.5
- tiles: bfloat16 [1024, 128, 128], P(('blk', 'row')), may hold values from 0 to 1
- tile_dest: int32 [1024], P(('blk', 'row')), may hold values from 0 to 63
- tile_src: int32 [1024], P(('blk', 'row')), may hold values from 0 to 127
- tile_fill: int32 [1024], P(('blk', 'row')), may hold values from 0 to 128
- out_degree: int32 [512, 128], P(('blk', 'row')), may hold values from 64 to 255
- dangling: int32 [512, 128], P(('blk', 'row')), may hold values 0 or 1
Outputs:
- rank: float32 [512, 128], P(('blk', 'row'))
- changes: float32 [2], replicated
Inputs may be any that keep to these rules, and one draw needn't show every extreme that they name: `tile_fill`: 0 marks an empty slot.
All inputs are finite; a program needn't handle non-finite values. No bound on the sum of `dangling` on one device may be relied on, other than what follows from the above.
Results may differ from a plain program's by a relative error of at most 0.0003.
Values may be sent and summed in bfloat16 or wider, within the bound.
A program may use at most 64 MiB of HBM per device.

v0:
```python
import jax
import jax.numpy as jnp
from jax import lax
from jax.sharding import PartitionSpec as P

ITERS = 2


damping = 0.85


def local(rank_start, tiles, tile_dest, tile_src, tile_fill, out_degree, dangling):
    share_tiles = rank_start.shape[0]
    page_total = lax.axis_size("blk") * lax.axis_size("row") * share_tiles * 128
    lane_index = jnp.arange(128, dtype=jnp.int32)
    column_mask = lane_index[None, :] < tile_fill[:, None]
    dangle = dangling.astype(jnp.float32)
    weight = (1.0 - dangle) / out_degree.astype(jnp.float32)
    rank = rank_start
    lost_mass = lax.psum(jnp.sum(rank * dangle), ("blk", "row"))
    change_list = []
    for iteration in range(ITERS):
        if iteration > 0:
            lost_mass = lax.psum(jnp.sum(rank * dangle), ("blk", "row"))
        scaled = (rank * weight).astype(jnp.bfloat16)
        block_part = lax.all_gather(scaled, "blk", axis=0, tiled=True)
        select = (
            tile_src[:, None] == jnp.arange(block_part.shape[0], dtype=jnp.int32)[None, :]
        ).astype(jnp.bfloat16)
        picked = jnp.dot(select, block_part, preferred_element_type=jnp.float32)
        sources = picked.astype(jnp.bfloat16)
        sources = jnp.where(column_mask, sources, jnp.zeros_like(sources))
        products = jnp.einsum("kij,kj->ki", tiles, sources, preferred_element_type=jnp.float32)
        dest_select = (
            tile_dest[:, None]
            == jnp.arange(lax.axis_size("row") * share_tiles, dtype=jnp.int32)[None, :]
        ).astype(jnp.float32)
        incoming = lax.psum_scatter(
            jnp.einsum("kd,ki->di", dest_select, products, precision=lax.Precision.HIGHEST),
            "row",
            scatter_dimension=0,
            tiled=True,
        )
        updated = damping * incoming + (1.0 - damping) + damping * lost_mass / page_total
        local_change = jnp.sum(jnp.abs(updated - rank))
        total_change = lax.psum(local_change, ("blk", "row"))
        change_list.append(total_change)
        rank = updated
    return (rank, jnp.stack(change_list))


def solution(mesh):
    placed = (
        P(("blk", "row"), None),
        P(("blk", "row"), None, None),
        P(("blk", "row")),
        P(("blk", "row")),
        P(("blk", "row")),
        P(("blk", "row"), None),
        P(("blk", "row"), None),
    )
    return jax.shard_map(
        local, mesh=mesh, in_specs=placed, out_specs=(P(("blk", "row"), None), P()), check_vma=False
    )
```

profile of v0, /device:TPU:0, one launch (start us, length us, event | category | flops | bytes accessed | tf_op | source)
XLA Modules:
  0.0 166.6 jit_solution(10766584483716675937)
XLA Ops:
  7.2 0.0 copy-start
  7.2 0.0 reduce-scatter.3.cloned.1.call-start
  7.2 1.4 multiply_convert_fusion.1
  8.6 0.0 copy-start.5
  8.6 0.0 copy-start.6
  8.6 10.7 %all_gather.6 = bf16[128,128]{1,0:T(8,128)(2,1)S(1)} all-gather(bf16[16,128]{1,0:T(8,128)(2,1)S(1)} %get-tuple-element.9), channel_id=1, replica_groups=mesh['blk'=8,'row'=4] {'blk'}, dimensions={0}, use_global_device_ids=true | all-gather | bytes 36864 | tf_op jit(solution)/shard_map/all_gather | solution.py:26
  19.4 0.0 copy-done.5
  19.4 0.0 copy-done.6
  19.4 0.2 fusion.1
  19.6 0.0 copy-done
  19.6 0.6 fusion.6
  20.2 0.0 copy-start.7
  20.2 0.7 copy-done.7
  20.9 0.9 fusion.9
  21.8 0.0 copy-start.1
  21.8 0.0 copy-start.2
  21.8 0.0 copy-start.3
  21.8 0.0 reduce-scatter.3.cloned.1.call-update
  21.8 0.0 reduce-scatter.5.cloned.1.call-start
  21.8 39.8 %psum.28 = f32[]{:T(128)} all-reduce(f32[]{:T(128)} %get-tuple-element.10), channel_id=1, replica_groups=mesh['blk'=8,'row'=4] {'blk','row'}, use_global_device_ids=true, to_apply=%region_2.3 | all-reduce | flops 1 | bytes 8 | tf_op jit(solution)/shard_map/psum | solution.py:20
  62.3 0.0 reduce-scatter.3.cloned.1.call-done
  62.3 0.0 copy-done.1
  62.3 0.0 copy-done.2
  62.4 0.0 copy-done.3
  62.4 1.3 abs_reduce_fusion.1
  63.7 10.1 %all_gather.7 = bf16[128,128]{1,0:T(8,128)(2,1)S(1)} all-gather(bf16[16,128]{1,0:T(8,128)(2,1)S(1)} %get-tuple-element.8), channel_id=1, replica_groups=mesh['blk'=8,'row'=4] {'blk'}, dimensions={0}, use_global_device_ids=true | all-gather | bytes 36864 | tf_op jit(solution)/shard_map/all_gather | solution.py:26
  73.7 0.2 fusion.3
  73.9 0.6 fusion.4
  74.6 0.9 fusion.8
  75.5 0.0 copy-start.4
  75.5 0.0 reduce-scatter.5.cloned.1.call-update
  75.5 39.5 %psum.29 = f32[]{:T(128)} all-reduce(f32[]{:T(128)} %get-tuple-element.3), channel_id=1, replica_groups=mesh['blk'=8,'row'=4] {'blk','row'}, use_global_device_ids=true, to_apply=%region_5.6 | all-reduce | flops 1 | bytes 8 | tf_op jit(solution)/shard_map/psum | solution.py:24
  115.6 0.0 reduce-scatter.5.cloned.1.call-done
  115.6 0.0 copy-done.4
  115.7 2.0 %abs_reduce_fusion = (f32[]{:T(128)}, f32[16,128]{1,0:T(8,128)}) fusion(f32[]{:T(128)S(6)} %div.10, f32[16,128]{1,0:T(8,128)S(1)} %copy-done.4, f32[]{:T(128)S(6)} %div.11, f32[16,128]{1,0:T(8,128)} %reduce-scatter.5.cloned.1.call-done), kind=kLoop, calls=%fused_computation.15 | loop fusion | flops 18431 | bytes 24588 | tf_op jit(solution)/shard_map/reduce_sum | solution.py:45
  117.6 40.4 %all-reduce = (f32[1]{0:T(128)}, f32[1]{0:T(128)}) all-reduce(f32[1]{0:T(128)} %bitcast.7, f32[1]{0:T(128)} %bitcast.6), channel_id=1, replica_groups=mesh['blk'=8,'row'=4] {'blk','row'}, use_global_device_ids=true, to_apply=%region_9.10 | all-reduce | flops 2 | bytes 16 | tf_op jit(solution)/shard_map/psum | solution.py:46
  158.0 1.8 %pad_maximum_fusion = f32[2]{0:T(128)} fusion(f32[1]{0:T(128)} %get-tuple-element.4, f32[1]{0:T(128)} %get-tuple-element.5), kind=kLoop, calls=%fused_computation.28 | loop fusion | flops 2 | bytes 16 | tf_op jit(solution)/shard_map/stack | solution.py:49
Async XLA Ops:
  7.2 12.4 %copy-start = (bf16[32,128,128]{2,1,0:T(8,128)(2,1)S(1)}, bf16[32,128,128]{2,1,0:T(8,128)(2,1)}, u32[]{:S(2)}) copy-start(bf16[32,128,128]{2,1,0:T(8,128)(2,1)} %param.8) | copy-start | bytes 3145732
  7.2 55.1 %reduce-scatter.3.cloned.1.call-start = ((), (), s32[]{:S(2)}) async-start(), calls=%async_computation.2 | async-start | bytes 40960 | tf_op jit(solution)/shard_map/reduce_scatter | solution.py:38
  8.6 10.7 %copy-start.5 = (s32[32]{0:T(128)S(1)}, s32[32]{0:T(128)}, u32[]{:S(2)}) copy-start(s32[32]{0:T(128)} %param.10) | copy-start | bytes 388
  8.6 10.7 %copy-start.6 = (s32[32]{0:T(128)S(1)}, s32[32]{0:T(128)}, u32[]{:S(2)}) copy-start(s32[32]{0:T(128)} %param.11) | copy-start | bytes 388
  20.2 0.7 copy-start.7
  21.8 40.6 %copy-start.1 = (f32[16,128]{1,0:T(8,128)S(1)}, f32[16,128]{1,0:T(8,128)}, u32[]{:S(2)}) copy-start(f32[16,128]{1,0:T(8,128)} %param.7) | copy-start | bytes 24580
  21.8 40.6 %copy-start.2 = (s32[16,128]{1,0:T(8,128)S(1)}, s32[16,128]{1,0:T(8,128)}, u32[]{:S(2)}) copy-start(s32[16,128]{1,0:T(8,128)} %param.12) | copy-start | bytes 24580
  21.8 40.6 %copy-start.3 = (s32[16,128]{1,0:T(8,128)S(1)}, s32[16,128]{1,0:T(8,128)}, u32[]{:S(2)}) copy-start(s32[16,128]{1,0:T(8,128)} %param.13) | copy-start | bytes 24580
  21.8 93.8 %reduce-scatter.5.cloned.1.call-start = ((), (), s32[]{:S(2)}) async-start(), calls=%async_computation.3 | async-start | bytes 40960 | tf_op jit(solution)/shard_map/reduce_scatter | solution.py:38
  75.5 40.2 %copy-start.4 = (f32[16,128]{1,0:T(8,128)S(1)}, f32[16,128]{1,0:T(8,128)}, u32[]{:S(2)}) copy-start(f32[16,128]{1,0:T(8,128)} %reduce-scatter.3.cloned.1.call-done) | copy-start | bytes 24580
Sparse Core Ops, SparseCore 0:
  21.9 19.4 reduce-scatter.2
  75.6 18.2 reduce-scatter.4
where the time goes:
time: 168 us; the launch traced here: 167 us
  blocking collectives  140 us (83%)
  between operations  15.4 us (9%)
  other arithmetic  6.49 us (4%)
  matrix products  3.45 us (2%)
    psum x2, blocking collectives, local(): lost_mass = lax.psum(jnp.sum(rank * dangle), ('blk', 'row'))  79.3 us
    psum x1, blocking collectives, local(): total_change = lax.psum(local_change, ('blk', 'row'))  40.4 us
    all_gather x2, blocking collectives, local(): block_part = lax.all_gather(scaled, 'blk', axis=0, tiled=True)  20.8 us
  transfers between devices with their start and end apart: 2, of which 0 were waited for; matrix products, arithmetic and copies ran while one was open for 0% of the time, Pallas kernels for 0%

commit v1 on v0

v1 whole, which is shorter than its diff:
```python
import functools

import jax
import jax.numpy as jnp
from jax import lax
from jax.experimental import pallas as pl
from jax.experimental.pallas import tpu as pltpu
from jax.sharding import PartitionSpec as P

ITERS = 2
UNROLL_LIMIT = 32

damping = 0.85


def each(count, body):
    if count <= UNROLL_LIMIT:
        for i in range(count):
            body(i)
    else:

        @pl.loop(0, count)
        def _(i):
            body(i)


def kernel(
    n_blk, n_row,
    rank_hbm, tiles_hbm, dest_hbm, src_hbm, fill_hbm, degree_hbm, dangling_hbm,
    rank_out, change_out,
    rank_v, tiles_v, degree_v, dangling_v, dest_s, src_s, fill_s,
    weight_v, dangle_v, spread_v, picked_v,
    pages, blk_stats, partial, shares, row_stats, in_sems, blk_sems, row_sems,
):
    b = lax.axis_index("blk")
    w = lax.axis_index("row")
    share, lanes = rank_v.shape
    slots = tiles_v.shape[0]
    page_total = n_blk * n_row * share * lanes

    def peer(axis, d):
        if axis == "blk":
            return {"blk": lax.rem(b + d, n_blk)}
        return {"row": lax.rem(w + d, n_row)}

    barrier = pltpu.get_barrier_semaphore()
    for axis, count in (("blk", n_blk), ("row", n_row)):
        each(count - 1, lambda i, axis=axis: pl.semaphore_signal(
            barrier, inc=1, device_id=peer(axis, i + 1),
            device_id_type=pl.DeviceIdType.MESH))

    loads = [
        pltpu.make_async_copy(source, target, in_sems.at[i])
        for i, (source, target) in enumerate((
            (rank_hbm, rank_v), (degree_hbm, degree_v), (dangling_hbm, dangling_v),
            (src_hbm, src_s), (dest_hbm, dest_s), (fill_hbm, fill_s), (tiles_hbm, tiles_v),
        ))
    ]
    for load in loads:
        load.start()
    for load in loads[:3]:
        load.wait()

    def send(axis, count, source, target, sems):
        def one(i):
            d = i + 1
            pltpu.make_async_remote_copy(
                src_ref=source(d), dst_ref=target.at[d],
                send_sem=sems.at[0], recv_sem=sems.at[1],
                device_id=peer(axis, d), device_id_type=pl.DeviceIdType.MESH,
            ).start()

        each(count - 1, one)

    def wait(count, target, sems, which):
        others = target.at[pl.ds(1, count - 1)]
        pltpu.make_async_copy(others, others, sems.at[which]).wait()

    sent = []

    def blk_send(source, target, sems):
        send("blk", n_blk, source, target, sems)
        sent.append((n_blk, target, sems))

    def row_send(source, target, sems):
        send("row", n_row, source, target, sems)
        sent.append((n_row, target, sems))

    def lane_sum(value):
        return jnp.sum(value, axis=0, keepdims=True)

    dangle = dangling_v[...].astype(jnp.float32)
    weight = (1.0 - dangle) / degree_v[...].astype(jnp.float32)
    weight_v[...] = weight
    dangle_v[...] = dangle
    rank = rank_v[...]
    pages[0, 0] = (rank * weight).astype(jnp.bfloat16)
    blk_stats[0, 0] = jnp.concatenate([lane_sum(rank * dangle), jnp.zeros((1, lanes), jnp.float32)], axis=0)
    pl.semaphore_wait(barrier, n_blk + n_row - 2)

    select = None
    for it in range(ITERS):
        blk_send(lambda d: pages.at[it, 0], pages.at[it], blk_sems.at[it, 0])
        blk_send(lambda d: blk_stats.at[it, 0], blk_stats.at[it], blk_sems.at[it, 1])

        if it == 0:
            for load in loads[3:6]:
                load.wait()
            slot_row = lax.broadcasted_iota(jnp.int32, (slots, n_blk * share), 0)
            slot_col = lax.broadcasted_iota(jnp.int32, (slots, n_blk * share), 1)
            source_row = jnp.zeros((slots, n_blk * share), jnp.int32)
            dest_row = lax.broadcasted_iota(jnp.int32, (n_row * share, lanes), 0)
            lane = lax.broadcasted_iota(jnp.int32, (n_row * share, lanes), 1)
            for k in range(slots):
                source = src_s[k]
                place = lax.rem(b - lax.div(source, share) + n_blk, n_blk) * share + lax.rem(source, share)
                source_row = jnp.where(slot_row == k, place, source_row)
                keep = (dest_row == dest_s[k]) & (lane < fill_s[k])
                spread_v[k] = jnp.where(keep, 1.0, 0.0)
            select = jnp.where(source_row == slot_col, 1.0, 0.0).astype(jnp.bfloat16)
            loads[6].wait()

        wait(n_blk, pages.at[it], blk_sems.at[it, 0], 1)
        picked_v[...] = jnp.dot(
            select, pages[it].reshape(n_blk * share, lanes), preferred_element_type=jnp.float32
        )
        total = jnp.zeros((n_row * share, lanes), jnp.float32)
        for k in range(slots):
            left = (spread_v[k] * picked_v[k:k + 1, :]).astype(jnp.bfloat16)
            total = total + lax.dot_general(
                left, tiles_v[k], (((1,), (1,)), ((), ())), preferred_element_type=jnp.float32
            )
        partial[it] = total.reshape(n_row, share, lanes)
        row_send(lambda d: partial.at[it, lax.rem(w + d, n_row)], shares.at[it], row_sems.at[it, 0])
        wait(n_blk, blk_stats.at[it], blk_sems.at[it, 1], 1)
        row_stats[it, 0] = jnp.sum(blk_stats[it], axis=0)
        row_send(lambda d: row_stats.at[it, 0], row_stats.at[it], row_sems.at[it, 1])
        own = partial[it, w]
        wait(n_row, row_stats.at[it], row_sems.at[it, 1], 1)
        stats = jnp.sum(jnp.sum(row_stats[it], axis=0), axis=1, keepdims=True)
        if it > 0:
            change_out[0:1, :] = jnp.broadcast_to(stats[1:2, :], (1, lanes))
        wait(n_row, shares.at[it], row_sems.at[it, 0], 1)
        incoming = own + jnp.sum(shares[it, 1:], axis=0)
        updated = damping * incoming + (1.0 - damping) + damping * stats[0:1, :] / page_total
        rank = rank_v[...]
        if it == 0:
            rank_v[...] = updated
            pages[it + 1, 0] = (updated * weight_v[...]).astype(jnp.bfloat16)
        else:
            rank_out[...] = updated
        blk_stats[it + 1, 0] = jnp.concatenate(
            [lane_sum(updated * dangle_v[...]), lane_sum(jnp.abs(updated - rank))], axis=0
        )

    blk_send(lambda d: blk_stats.at[ITERS, 0], blk_stats.at[ITERS], blk_sems.at[ITERS, 1])
    wait(n_blk, blk_stats.at[ITERS], blk_sems.at[ITERS, 1], 1)
    row_stats[ITERS, 0] = jnp.sum(blk_stats[ITERS], axis=0)
    row_send(lambda d: row_stats.at[ITERS, 0], row_stats.at[ITERS], row_sems.at[ITERS, 1])
    wait(n_row, row_stats.at[ITERS], row_sems.at[ITERS, 1], 1)
    stats = jnp.sum(jnp.sum(row_stats[ITERS], axis=0), axis=1, keepdims=True)
    change_out[1:2, :] = jnp.broadcast_to(stats[1:2, :], (1, lanes))
    for count, target, sems in sent:
        wait(count, target, sems, 0)


def solution(mesh):
    placed = (
        P(("blk", "row"), None),
        P(("blk", "row"), None, None),
        P(("blk", "row")),
        P(("blk", "row")),
        P(("blk", "row")),
        P(("blk", "row"), None),
        P(("blk", "row"), None),
    )
    n_blk, n_row = mesh.shape["blk"], mesh.shape["row"]

    def local(rank_start, tiles, tile_dest, tile_src, tile_fill, out_degree, dangling):
        share, lanes = rank_start.shape
        slots = tiles.shape[0]
        rank, changes = pl.pallas_call(
            functools.partial(kernel, n_blk, n_row),
            out_shape=(
                jax.ShapeDtypeStruct((share, lanes), jnp.float32),
                jax.ShapeDtypeStruct((2, lanes), jnp.float32),
            ),
            in_specs=[pl.BlockSpec(memory_space=pl.ANY)] * 7,
            out_specs=(pl.BlockSpec(memory_space=pltpu.VMEM),) * 2,
            scratch_shapes=[
                pltpu.VMEM((share, lanes), jnp.float32),
                pltpu.VMEM(tiles.shape, jnp.bfloat16),
                pltpu.VMEM((share, lanes), jnp.int32),
                pltpu.VMEM((share, lanes), jnp.int32),
                pltpu.SMEM((slots,), jnp.int32),
                pltpu.SMEM((slots,), jnp.int32),
                pltpu.SMEM((slots,), jnp.int32),
                pltpu.VMEM((share, lanes), jnp.float32),
                pltpu.VMEM((share, lanes), jnp.float32),
                pltpu.VMEM((slots, n_row * share, lanes), jnp.float32),
                pltpu.VMEM((slots, lanes), jnp.float32),
                pltpu.VMEM((ITERS, n_blk, share, lanes), jnp.bfloat16),
                pltpu.VMEM((ITERS + 1, n_blk, 2, lanes), jnp.float32),
                pltpu.VMEM((ITERS, n_row, share, lanes), jnp.float32),
                pltpu.VMEM((ITERS, n_row, share, lanes), jnp.float32),
                pltpu.VMEM((ITERS + 1, n_row, 2, lanes), jnp.float32),
                pltpu.SemaphoreType.DMA((7,)),
                pltpu.SemaphoreType.DMA((ITERS + 1, 2, 2)),
                pltpu.SemaphoreType.DMA((ITERS + 1, 2, 2)),
            ],
            compiler_params=pltpu.CompilerParams(collective_id=0, has_side_effects=True),
        )(rank_start, tiles, tile_dest, tile_src, tile_fill, out_degree, dangling)
        return rank, changes[:, 0]

    return jax.shard_map(
        local, mesh=mesh, in_specs=placed, out_specs=(P(("blk", "row"), None), P()), check_vma=False
    )
```

time: 168 us -> 32.5 us (0.19)
  blocking collectives: 140 us -> 0 us
  Pallas kernels: 0 us -> 29 us
  between operations: 15.4 us -> 0.65 us
  other arithmetic: 6.49 us -> 0 us
  matrix products: 3.45 us -> 0 us
  local copies, waits for them, and re-layouts: 0.71 us -> 2.57 us
    psum x3 -> x0, blocking collectives: 120 us -> none  [the longest x2 79.3 us: local(): lost_mass = lax.psum(jnp.sum(rank * dangle), ('blk', 'row'))]
    pallas_call x0 -> x1, Pallas kernels: none -> 29 us  [local(): pl.pallas_call(functools.partial(kernel, n_blk, n_row), out_shape=(jax.Sh...]
    all_gather x2 -> x0, blocking collectives: 20.8 us -> none  [local(): block_part = lax.all_gather(scaled, 'blk', axis=0, tiled=True)]
    dot_general x6 -> x0, matrix products: 3.45 us -> none  [the longest x2 1.8 us: local(): jnp.einsum('kd,ki->di', dest_select, products, precision=lax.Precision.HI...]
    reduce_sum x2 -> x0, other arithmetic: 3.3 us -> none  [local(): local_change = jnp.sum(jnp.abs(updated - rank))]
    another operation x1 -> x0, other arithmetic: 1.78 us -> none  [local(): return (rank, jnp.stack(change_list))]
  transfers between devices with their start and end apart: 2 -> 0, of which waited for: 0 -> 0; matrix products, arithmetic and copies ran while one was open for 0% -> 0% of each run, Pallas kernels for 0% -> 0%
where the time goes in v1:
time: 32.5 us; the launch traced here: 32.2 us
  Pallas kernels  29 us (89%)
  local copies, waits for them, and re-layouts  2.57 us (8%)
  between operations  0.65 us (2%)
    pallas_call x1, Pallas kernels, local(): pl.pallas_call(functools.partial(kernel, n_blk, n_row), out_shape=(jax.Sh...  29 us
    unnamed x3, local copies, waits for them, and re-layouts  1.95 us

profile of v1, /device:TPU:0, one launch (start us, length us, event | category | flops | bytes accessed | tf_op | source)
XLA Modules:
  0.0 32.2 jit_solution(7440371097515180183)
XLA Ops:
  0.6 29.0 %shard_map.86 = (f32[16,128]{1,0:T(8,128)}, f32[2,128]{1,0:T(2,128)}) custom-call(f32[16,128]{1,0:T(8,128)} %rank_hbm.1, bf16[32,128,128]{2,1,0:T(8,128)(2,1)} %tiles_hbm.1, s32[32]{0:T(128)} %dest_hbm.1, s32[32]{0:T(128)} %src_hbm.1, s32[32]{0:T(128)} %fill_hbm.1, s32[16,128]{1,0:T(8,128)} %degree_hbm.1, s32[16,128]{1,0:T(8,128)} %dangling_hbm.1), custom_call_target="tpu_custom_call" | custom-call | tf_op jit(solution)/shard_map/pallas_call | solution.py:182
  29.6 0.0 copy-start
  29.6 0.7 %copy-done = f32[2,128]{1,0:T(2,128)S(1)} copy-done((f32[2,128]{1,0:T(2,128)S(1)}, f32[2,128]{1,0:T(2,128)}, u32[]{:S(2)}) %copy-start) | copy-done | bytes 1048
  30.3 0.6 %slice_reduce_fusion = f32[2]{0:T(128)} fusion(f32[2,128]{1,0:T(2,128)S(1)} %copy-done), kind=kLoop, calls=%fused_computation | loop fusion | bytes 16 | tf_op jit(solution)/shard_map/slice | solution.py:213
  30.9 1.3 %copy.10 = f32[16,128]{1,0:T(8,128)} copy(f32[16,128]{1,0:T(8,128)} %get-tuple-element.8) | data formatting | bytes 16384
Async XLA Ops:
  29.6 0.7 %copy-start = (f32[2,128]{1,0:T(2,128)S(1)}, f32[2,128]{1,0:T(2,128)}, u32[]{:S(2)}) copy-start(f32[2,128]{1,0:T(2,128)} %get-tuple-element.5) | copy-start | bytes 3076

commit v2 on v1

--- a/solution.py
+++ b/solution.py
@@ -24,13 +24,24 @@
             body(i)
 
 
+def finish(rank_ref, change_ref, rank_hbm, change_hbm, change_s, sems):
+    write_rank = pltpu.make_async_copy(rank_ref, rank_hbm, sems.at[0])
+    write_rank.start()
+    for i in range(ITERS):
+        change_s[i] = jnp.max(change_ref[i:i + 1, :])
+    write_change = pltpu.make_async_copy(change_s, change_hbm, sems.at[1])
+    write_change.start()
+    write_rank.wait()
+    write_change.wait()
+
+
 def kernel(
     n_blk, n_row,
     rank_hbm, tiles_hbm, dest_hbm, src_hbm, fill_hbm, degree_hbm, dangling_hbm,
     rank_out, change_out,
     rank_v, tiles_v, degree_v, dangling_v, dest_s, src_s, fill_s,
     weight_v, dangle_v, spread_v, picked_v,
-    pages, blk_stats, partial, shares, row_stats, in_sems, blk_sems, row_sems,
+    pages, blk_stats, partial, shares, row_stats, last_stats, in_sems, blk_sems, row_sems, last_sems,
 ):
     b = lax.axis_index("blk")
     w = lax.axis_index("row")
@@ -41,7 +52,9 @@
     def peer(axis, d):
         if axis == "blk":
             return {"blk": lax.rem(b + d, n_blk)}
-        return {"row": lax.rem(w + d, n_row)}
+        if axis == "row":
+            return {"row": lax.rem(w + d, n_row)}
+        return {"blk": lax.rem(b + d // n_row, n_blk), "row": lax.rem(w + d % n_row, n_row)}
 
     barrier = pltpu.get_barrier_semaphore()
     for axis, count in (("blk", n_blk), ("row", n_row)):
@@ -124,42 +137,44 @@
         picked_v[...] = jnp.dot(
             select, pages[it].reshape(n_blk * share, lanes), preferred_element_type=jnp.float32
         )
-        total = jnp.zeros((n_row * share, lanes), jnp.float32)
-        for k in range(slots):
-            left = (spread_v[k] * picked_v[k:k + 1, :]).astype(jnp.bfloat16)
-            total = total + lax.dot_general(
-                left, tiles_v[k], (((1,), (1,)), ((), ())), preferred_element_type=jnp.float32
-            )
-        partial[it] = total.reshape(n_row, share, lanes)
-        row_send(lambda d: partial.at[it, lax.rem(w + d, n_row)], shares.at[it], row_sems.at[it, 0])
         wait(n_blk, blk_stats.at[it], blk_sems.at[it, 1], 1)
         row_stats[it, 0] = jnp.sum(blk_stats[it], axis=0)
         row_send(lambda d: row_stats.at[it, 0], row_stats.at[it], row_sems.at[it, 1])
+        totals = [jnp.zeros((n_row * share, lanes), jnp.float32) for _ in range(2)]
+        for k in range(0, slots, 2):
+            left = jnp.concatenate([spread_v[k + i] * picked_v[k + i:k + i + 1, :] for i in range(2)], axis=1)
+            right = jnp.concatenate([tiles_v[k + i] for i in range(2)], axis=1)
+            half = k // 2 % 2
+            totals[half] = totals[half] + lax.dot_general(
+                left.astype(jnp.bfloat16), right, (((1,), (1,)), ((), ())), preferred_element_type=jnp.float32
+            )
+        partial[it] = (totals[0] + totals[1]).reshape(n_row, share, lanes)
+        row_send(lambda d: partial.at[it, lax.rem(w + d, n_row)], shares.at[it], row_sems.at[it, 0])
         own = partial[it, w]
         wait(n_row, row_stats.at[it], row_sems.at[it, 1], 1)
         stats = jnp.sum(jnp.sum(row_stats[it], axis=0), axis=1, keepdims=True)
         if it > 0:
             change_out[0:1, :] = jnp.broadcast_to(stats[1:2, :], (1, lanes))
+        base = (1.0 - damping) + damping * stats[0:1, :] / page_total
         wait(n_row, shares.at[it], row_sems.at[it, 0], 1)
         incoming = own + jnp.sum(shares[it, 1:], axis=0)
-        updated = damping * incoming + (1.0 - damping) + damping * stats[0:1, :] / page_total
+        updated = damping * incoming + base
         rank = rank_v[...]
         if it == 0:
             rank_v[...] = updated
             pages[it + 1, 0] = (updated * weight_v[...]).astype(jnp.bfloat16)
+            blk_stats[it + 1, 0] = jnp.concatenate(
+                [lane_sum(updated * dangle_v[...]), lane_sum(jnp.abs(updated - rank))], axis=0
+            )
         else:
+            last_stats[0] = lane_sum(jnp.abs(updated - rank))
             rank_out[...] = updated
-        blk_stats[it + 1, 0] = jnp.concatenate(
-            [lane_sum(updated * dangle_v[...]), lane_sum(jnp.abs(updated - rank))], axis=0
-        )
-
-    blk_send(lambda d: blk_stats.at[ITERS, 0], blk_stats.at[ITERS], blk_sems.at[ITERS, 1])
-    wait(n_blk, blk_stats.at[ITERS], blk_sems.at[ITERS, 1], 1)
-    row_stats[ITERS, 0] = jnp.sum(blk_stats[ITERS], axis=0)
-    row_send(lambda d: row_stats.at[ITERS, 0], row_stats.at[ITERS], row_sems.at[ITERS, 1])
-    wait(n_row, row_stats.at[ITERS], row_sems.at[ITERS, 1], 1)
-    stats = jnp.sum(jnp.sum(row_stats[ITERS], axis=0), axis=1, keepdims=True)
-    change_out[1:2, :] = jnp.broadcast_to(stats[1:2, :], (1, lanes))
+
+    send("all", n_blk * n_row, lambda d: last_stats.at[0], last_stats, last_sems)
+    sent.append((n_blk * n_row, last_stats, last_sems))
+    wait(n_blk * n_row, last_stats, last_sems, 1)
+    last = jnp.sum(jnp.sum(last_stats[...], axis=0), axis=1, keepdims=True)
+    change_out[1:2, :] = jnp.broadcast_to(last, (1, lanes))
     for count, target, sems in sent:
         wait(count, target, sems, 0)
 
@@ -182,8 +197,8 @@
         rank, changes = pl.pallas_call(
             functools.partial(kernel, n_blk, n_row),
             out_shape=(
-                jax.ShapeDtypeStruct((share, lanes), jnp.float32),
-                jax.ShapeDtypeStruct((2, lanes), jnp.float32),
+                pltpu.VMEM((share, lanes), jnp.float32),
+                pltpu.VMEM((ITERS, lanes), jnp.float32),
             ),
             in_specs=[pl.BlockSpec(memory_space=pl.ANY)] * 7,
             out_specs=(pl.BlockSpec(memory_space=pltpu.VMEM),) * 2,
@@ -200,17 +215,29 @@
                 pltpu.VMEM((slots, n_row * share, lanes), jnp.float32),
                 pltpu.VMEM((slots, lanes), jnp.float32),
                 pltpu.VMEM((ITERS, n_blk, share, lanes), jnp.bfloat16),
-                pltpu.VMEM((ITERS + 1, n_blk, 2, lanes), jnp.float32),
+                pltpu.VMEM((ITERS, n_blk, 2, lanes), jnp.float32),
                 pltpu.VMEM((ITERS, n_row, share, lanes), jnp.float32),
                 pltpu.VMEM((ITERS, n_row, share, lanes), jnp.float32),
-                pltpu.VMEM((ITERS + 1, n_row, 2, lanes), jnp.float32),
+                pltpu.VMEM((ITERS, n_row, 2, lanes), jnp.float32),
+                pltpu.VMEM((n_blk * n_row, 1, lanes), jnp.float32),
                 pltpu.SemaphoreType.DMA((7,)),
-                pltpu.SemaphoreType.DMA((ITERS + 1, 2, 2)),
-                pltpu.SemaphoreType.DMA((ITERS + 1, 2, 2)),
+                pltpu.SemaphoreType.DMA((ITERS, 2, 2)),
+                pltpu.SemaphoreType.DMA((ITERS, 2, 2)),
+                pltpu.SemaphoreType.DMA((2,)),
             ],
             compiler_params=pltpu.CompilerParams(collective_id=0, has_side_effects=True),
         )(rank_start, tiles, tile_dest, tile_src, tile_fill, out_degree, dangling)
-        return rank, changes[:, 0]
+        return tuple(pl.pallas_call(
+            finish,
+            out_shape=(
+                jax.ShapeDtypeStruct((share, lanes), jnp.float32),
+                jax.ShapeDtypeStruct((ITERS,), jnp.float32),
+            ),
+            in_specs=[pl.BlockSpec(memory_space=pltpu.VMEM)] * 2,
+            out_specs=(pl.BlockSpec(memory_space=pl.ANY),) * 2,
+            scratch_shapes=[pltpu.SMEM((ITERS,), jnp.float32), pltpu.SemaphoreType.DMA((2,))],
+            compiler_params=pltpu.CompilerParams(vmem_limit_bytes=1 << 20),
+        )(rank, changes))
 
     return jax.shard_map(
         local, mesh=mesh, in_specs=placed, out_specs=(P(("blk", "row"), None), P()), check_vma=False

time: 32.5 us -> 26.4 us (0.81)
  Pallas kernels: 29 us -> 25.5 us
  local copies, waits for them, and re-layouts: 2.57 us -> 0 us
    pallas_call x1 -> x2, Pallas kernels: 29 us -> 25.5 us  [the longest x1 24.9 us: local(): pl.pallas_call(functools.partial(kernel, n_blk, n_row), out_shape=(pltpu....]
    unnamed x3 -> x0, local copies, waits for them, and re-layouts: 1.95 us -> none
    slice x1 -> x0, local copies, waits for them, and re-layouts: 0.63 us -> none  [local(): return (rank, changes[:, 0])]
where the time goes in v2:
time: 26.4 us; the launch traced here: 26.2 us
  Pallas kernels  25.5 us (97%)
  between operations  0.64 us (2%)
    pallas_call x1, Pallas kernels, local(): pl.pallas_call(functools.partial(kernel, n_blk, n_row), out_shape=(pltpu....  24.9 us
    pallas_call x1, Pallas kernels, local(): pl.pallas_call(finish, out_shape=(jax.ShapeDtypeStruct((share, lanes), jn...  0.65 us

profile of v2, /device:TPU:0, one launch (start us, length us, event | category | flops | bytes accessed | tf_op | source)
XLA Modules:
  0.0 26.2 jit_solution(6221485569205922918)
XLA Ops:
  0.6 24.9 %shard_map.86 = (f32[16,128]{1,0:T(8,128)S(1)}, f32[2,128]{1,0:T(2,128)S(1)}) custom-call(f32[16,128]{1,0:T(8,128)} %rank_hbm.1, bf16[32,128,128]{2,1,0:T(8,128)(2,1)} %tiles_hbm.1, s32[32]{0:T(128)} %dest_hbm.1, s32[32]{0:T(128)} %src_hbm.1, s32[32]{0:T(128)} %fill_hbm.1, s32[16,128]{1,0:T(8,128)} %degree_hbm.1, s32[16,128]{1,0:T(8,128)} %dangling_hbm.1), custom_call_target="tpu_custom_call" | custom-call | tf_op jit(solution)/shard_map/pallas_call | solution.py:197
  25.5 0.7 %shard_map.87 = (f32[16,128]{1,0:T(8,128)}, f32[2]{0:T(128)}) custom-call(f32[16,128]{1,0:T(8,128)S(1)} %get-tuple-element.4.rank_ref, f32[2,128]{1,0:T(2,128)S(1)} %get-tuple-element.5.change_ref), custom_call_target="tpu_custom_call" | custom-call | tf_op jit(solution)/shard_map/pallas_call | solution.py:230

commit v3 on v2

--- a/solution.py
+++ b/solution.py
@@ -39,7 +39,7 @@
     n_blk, n_row,
     rank_hbm, tiles_hbm, dest_hbm, src_hbm, fill_hbm, degree_hbm, dangling_hbm,
     rank_out, change_out,
-    rank_v, tiles_v, degree_v, dangling_v, dest_s, src_s, fill_s,
+    rank_v, tiles_v, turned_v, degree_v, dangling_v, dest_s, src_s, fill_s,
     weight_v, dangle_v, spread_v, picked_v,
     pages, blk_stats, partial, shares, row_stats, last_stats, in_sems, blk_sems, row_sems, last_sems,
 ):
@@ -132,6 +132,8 @@
                 spread_v[k] = jnp.where(keep, 1.0, 0.0)
             select = jnp.where(source_row == slot_col, 1.0, 0.0).astype(jnp.bfloat16)
             loads[6].wait()
+            for k in range(slots):
+                turned_v[k] = tiles_v[k].T
 
         wait(n_blk, pages.at[it], blk_sems.at[it, 0], 1)
         picked_v[...] = jnp.dot(
@@ -143,10 +145,10 @@
         totals = [jnp.zeros((n_row * share, lanes), jnp.float32) for _ in range(2)]
         for k in range(0, slots, 2):
             left = jnp.concatenate([spread_v[k + i] * picked_v[k + i:k + i + 1, :] for i in range(2)], axis=1)
-            right = jnp.concatenate([tiles_v[k + i] for i in range(2)], axis=1)
+            right = jnp.concatenate([turned_v[k + i] for i in range(2)], axis=0)
             half = k // 2 % 2
             totals[half] = totals[half] + lax.dot_general(
-                left.astype(jnp.bfloat16), right, (((1,), (1,)), ((), ())), preferred_element_type=jnp.float32
+                left.astype(jnp.bfloat16), right, (((1,), (0,)), ((), ())), preferred_element_type=jnp.float32
             )
         partial[it] = (totals[0] + totals[1]).reshape(n_row, share, lanes)
         row_send(lambda d: partial.at[it, lax.rem(w + d, n_row)], shares.at[it], row_sems.at[it, 0])
@@ -204,6 +206,7 @@
             out_specs=(pl.BlockSpec(memory_space=pltpu.VMEM),) * 2,
             scratch_shapes=[
                 pltpu.VMEM((share, lanes), jnp.float32),
+                pltpu.VMEM(tiles.shape, jnp.bfloat16),
                 pltpu.VMEM(tiles.shape, jnp.bfloat16),
                 pltpu.VMEM((share, lanes), jnp.int32),
                 pltpu.VMEM((share, lanes), jnp.int32),

time: 26.4 us -> 25.6 us (0.970)
  Pallas kernels: 25.5 us -> 24.8 us
    pallas_call x1, Pallas kernels: 24.9 us -> 24.1 us  [local(): pl.pallas_call(functools.partial(kernel, n_blk, n_row), out_shape=(pltpu....]
where the time goes in v3:
time: 25.6 us; the launch traced here: 25.4 us
  Pallas kernels  24.8 us (97%)
  between operations  0.64 us (2%)
    pallas_call x1, Pallas kernels, local(): pl.pallas_call(functools.partial(kernel, n_blk, n_row), out_shape=(pltpu....  24.1 us
    pallas_call x1, Pallas kernels, local(): pl.pallas_call(finish, out_shape=(jax.ShapeDtypeStruct((share, lanes), jn...  0.65 us

profile of v3, /device:TPU:0, one launch (start us, length us, event | category | flops | bytes accessed | tf_op | source)
XLA Modules:
  0.0 25.4 jit_solution(7974205158888428180)
XLA Ops:
  0.6 24.1 %shard_map.86 = (f32[16,128]{1,0:T(8,128)S(1)}, f32[2,128]{1,0:T(2,128)S(1)}) custom-call(f32[16,128]{1,0:T(8,128)} %rank_hbm.1, bf16[32,128,128]{2,1,0:T(8,128)(2,1)} %tiles_hbm.1, s32[32]{0:T(128)} %dest_hbm.1, s32[32]{0:T(128)} %src_hbm.1, s32[32]{0:T(128)} %fill_hbm.1, s32[16,128]{1,0:T(8,128)} %degree_hbm.1, s32[16,128]{1,0:T(8,128)} %dangling_hbm.1), custom_call_target="tpu_custom_call" | custom-call | tf_op jit(solution)/shard_map/pallas_call | solution.py:199
  24.8 0.7 %shard_map.87 = (f32[16,128]{1,0:T(8,128)}, f32[2]{0:T(128)}) custom-call(f32[16,128]{1,0:T(8,128)S(1)} %get-tuple-element.4.rank_ref, f32[2,128]{1,0:T(2,128)S(1)} %get-tuple-element.5.change_ref), custom_call_target="tpu_custom_call" | custom-call | tf_op jit(solution)/shard_map/pallas_call | solution.py:233

commit v4 on v3

--- a/solution.py
+++ b/solution.py
@@ -24,15 +24,15 @@
             body(i)
 
 
-def finish(rank_ref, change_ref, rank_hbm, change_hbm, change_s, sems):
-    write_rank = pltpu.make_async_copy(rank_ref, rank_hbm, sems.at[0])
-    write_rank.start()
-    for i in range(ITERS):
-        change_s[i] = jnp.max(change_ref[i:i + 1, :])
-    write_change = pltpu.make_async_copy(change_s, change_hbm, sems.at[1])
-    write_change.start()
-    write_rank.wait()
-    write_change.wait()
+def finish(rank_ref, change_ref, rank_hbm, change_hbm, sems):
+    writes = [
+        pltpu.make_async_copy(source, target, sems.at[i])
+        for i, (source, target) in enumerate(((rank_ref, rank_hbm), (change_ref, change_hbm)))
+    ]
+    for write in writes:
+        write.start()
+    for write in writes:
+        write.wait()
 
 
 def kernel(
@@ -112,6 +112,8 @@
     pl.semaphore_wait(barrier, n_blk + n_row - 2)
 
     select = None
+    order = lax.broadcasted_iota(jnp.int32, (1, ITERS), 1)
+    moves = jnp.zeros((1, ITERS), jnp.float32)
     for it in range(ITERS):
         blk_send(lambda d: pages.at[it, 0], pages.at[it], blk_sems.at[it, 0])
         blk_send(lambda d: blk_stats.at[it, 0], blk_stats.at[it], blk_sems.at[it, 1])
@@ -156,7 +158,7 @@
         wait(n_row, row_stats.at[it], row_sems.at[it, 1], 1)
         stats = jnp.sum(jnp.sum(row_stats[it], axis=0), axis=1, keepdims=True)
         if it > 0:
-            change_out[0:1, :] = jnp.broadcast_to(stats[1:2, :], (1, lanes))
+            moves = jnp.where(order == it - 1, stats[1:2, :], moves)
         base = (1.0 - damping) + damping * stats[0:1, :] / page_total
         wait(n_row, shares.at[it], row_sems.at[it, 0], 1)
         incoming = own + jnp.sum(shares[it, 1:], axis=0)
@@ -176,7 +178,7 @@
     sent.append((n_blk * n_row, last_stats, last_sems))
     wait(n_blk * n_row, last_stats, last_sems, 1)
     last = jnp.sum(jnp.sum(last_stats[...], axis=0), axis=1, keepdims=True)
-    change_out[1:2, :] = jnp.broadcast_to(last, (1, lanes))
+    change_out[...] = jnp.where(order == ITERS - 1, last, moves)
     for count, target, sems in sent:
         wait(count, target, sems, 0)
 
@@ -200,7 +202,7 @@
             functools.partial(kernel, n_blk, n_row),
             out_shape=(
                 pltpu.VMEM((share, lanes), jnp.float32),
-                pltpu.VMEM((ITERS, lanes), jnp.float32),
+                pltpu.VMEM((1, ITERS), jnp.float32),
             ),
             in_specs=[pl.BlockSpec(memory_space=pl.ANY)] * 7,
             out_specs=(pl.BlockSpec(memory_space=pltpu.VMEM),) * 2,
@@ -230,17 +232,18 @@
             ],
             compiler_params=pltpu.CompilerParams(collective_id=0, has_side_effects=True),
         )(rank_start, tiles, tile_dest, tile_src, tile_fill, out_degree, dangling)
-        return tuple(pl.pallas_call(
+        rank, changes = pl.pallas_call(
             finish,
             out_shape=(
                 jax.ShapeDtypeStruct((share, lanes), jnp.float32),
-                jax.ShapeDtypeStruct((ITERS,), jnp.float32),
+                jax.ShapeDtypeStruct((1, ITERS), jnp.float32),
             ),
             in_specs=[pl.BlockSpec(memory_space=pltpu.VMEM)] * 2,
             out_specs=(pl.BlockSpec(memory_space=pl.ANY),) * 2,
-            scratch_shapes=[pltpu.SMEM((ITERS,), jnp.float32), pltpu.SemaphoreType.DMA((2,))],
+            scratch_shapes=[pltpu.SemaphoreType.DMA((2,))],
             compiler_params=pltpu.CompilerParams(vmem_limit_bytes=1 << 20),
-        )(rank, changes))
+        )(rank, changes)
+        return rank, changes.reshape(ITERS)
 
     return jax.shard_map(
         local, mesh=mesh, in_specs=placed, out_specs=(P(("blk", "row"), None), P()), check_vma=False

time: 25.6 us -> 25.6 us (level)
  no operation moved by 1% of the time
where the time goes in v4:
time: 25.6 us; the launch traced here: 25.4 us
  Pallas kernels  24.8 us (97%)
  between operations  0.64 us (2%)
    pallas_call x1, Pallas kernels, local(): pl.pallas_call(functools.partial(kernel, n_blk, n_row), out_shape=(pltpu....  24.1 us
    pallas_call x1, Pallas kernels, local(): pl.pallas_call(finish, out_shape=(jax.ShapeDtypeStruct((share, lanes), jn...  0.62 us

profile of v4, /device:TPU:0, one launch (start us, length us, event | category | flops | bytes accessed | tf_op | source)
XLA Modules:
  0.0 25.4 jit_solution(17913832487712433161)
XLA Ops:
  0.6 24.1 %shard_map.86 = (f32[16,128]{1,0:T(8,128)S(1)}, f32[1,2]{1,0:T(1,128)S(1)}) custom-call(f32[16,128]{1,0:T(8,128)} %rank_hbm.1, bf16[32,128,128]{2,1,0:T(8,128)(2,1)} %tiles_hbm.1, s32[32]{0:T(128)} %dest_hbm.1, s32[32]{0:T(128)} %src_hbm.1, s32[32]{0:T(128)} %fill_hbm.1, s32[16,128]{1,0:T(8,128)} %degree_hbm.1, s32[16,128]{1,0:T(8,128)} %dangling_hbm.1), custom_call_target="tpu_custom_call" | custom-call | tf_op jit(solution)/shard_map/pallas_call | solution.py:201
  24.8 0.6 %shard_map.87 = (f32[16,128]{1,0:T(8,128)}, f32[1,2]{1,0:T(1,128)}) custom-call(f32[16,128]{1,0:T(8,128)S(1)} %get-tuple-element.6.rank_ref, f32[1,2]{1,0:T(1,128)S(1)} %get-tuple-element.7.change_ref), custom_call_target="tpu_custom_call" | custom-call | tf_op jit(solution)/shard_map/pallas_call | solution.py:235
